TPU v7x, 32 devices: a whole 2x2x4 slice. The times are simulated.
32 devices in a mesh: bucket: 4 (over y, x), seq: 8 (over z, core).
Axes of the slice: x: 2, y: 2, z: 4, core: 2. Of those that a mesh axis runs over, the one named last changes fastest.
Arguments:
- queries: bfloat16 [4, 448, 1536], P('bucket', 'seq'), may hold values from -45 to 45, as said below
- keys: bfloat16 [4, 448, 1536], P('bucket', 'seq'), may hold values from -5 to 5
- values: bfloat16 [4, 448, 1536], P('bucket', 'seq'), may hold values from -6 to 6
- bucket_lens: int32 [4], P('bucket'), may hold values from 224 to 392
- gate: float32 [4, 3072], P('bucket'), may hold values from 0.5 to 2
- out_weight: bfloat16 [1536, 3072], P(None, 'bucket'), may hold values from -0.15625 to 0.15625
Outputs:
- gated_out: bfloat16 [4, 448, 3072], P('bucket', 'seq')
Inputs may be any that keep to these rules, and one draw needn't show every extreme that they name: queries of a few tokens in a bucket may be strong multiples of some keys.
All inputs are finite; a program needn't handle non-finite values.
Results may differ from a plain program's by a relative error of at most 0.013.
Values may be sent and summed in bfloat16 or wider, within the bound.
No kernel may reach another device: no remote copies, remote signals or barrier semaphores. Data moves between devices by JAX's collectives and lax.ppermute only.
A program may use at most 192 MiB of HBM per device.

v0:
```python
import math

import jax
import jax.numpy as jnp
from jax import lax
from jax.experimental import pallas as pl
from jax.experimental.pallas import tpu as pltpu
from jax.sharding import PartitionSpec as P


HEAD_DIM = 128
NEG_FILL = -1e30

VMEM = pl.BlockSpec(memory_space=pltpu.VMEM)
SMEM = pl.BlockSpec(memory_space=pltpu.SMEM)


def cut_pieces(row, queries, keys, values, outer):
    rows, width = queries.shape
    share = width // outer

    def body(row_ref, q_ref, k_ref, v_ref, *outs):
        for k in range(outer):
            cut = pl.ds(pl.multiple_of((row_ref[0] ^ k) * share, HEAD_DIM), share)
            outs[k][:, :share] = k_ref[:, cut]
            outs[k][:, share:] = v_ref[:, cut]
            outs[outer + k][...] = q_ref[:, cut]

    shapes = [jax.ShapeDtypeStruct((rows, 2 * share), queries.dtype)] * outer
    shapes += [jax.ShapeDtypeStruct((rows, share), queries.dtype)] * outer
    out = pl.pallas_call(
        body, out_shape=shapes, in_specs=[SMEM, VMEM, VMEM, VMEM], out_specs=[VMEM] * (2 * outer),
        name="cut_pieces",
    )(row, queries, keys, values)
    return out[:outer], out[outer:]


def attend_pieces(usable, queries, pairs):
    rows_here, share = queries[0].shape
    outer = len(queries)

    def body(usable_ref, *refs):
        q_refs, pair_refs = refs[:outer], refs[outer : outer + len(pairs)]
        outs = refs[outer + len(pairs) :]
        keep = usable_ref[...] > 0
        scores, values = [], []
        for head in range(share // HEAD_DIM):
            cut = slice(head * HEAD_DIM, (head + 1) * HEAD_DIM)
            vcut = slice(share + head * HEAD_DIM, share + (head + 1) * HEAD_DIM)
            query = jnp.concatenate([r[:, cut] for r in q_refs], axis=0)
            key = jnp.concatenate([r[:, cut] for r in pair_refs], axis=0)
            values.append(jnp.concatenate([r[:, vcut] for r in pair_refs], axis=0))
            score = lax.dot_general(
                query, key, (((1,), (1,)), ((), ())), preferred_element_type=jnp.float32
            ) * HEAD_DIM ** (-0.5)
            scores.append(jnp.where(keep, score, NEG_FILL))
        weights = [jnp.exp(s - jnp.max(s, axis=1, keepdims=True)) for s in scores]
        results = []
        for weight, value in zip(weights, values):
            total = jnp.sum(weight, axis=1, keepdims=True)
            out = jnp.dot(weight.astype(jnp.bfloat16), value, preferred_element_type=jnp.float32)
            results.append((out * (1.0 / total)).astype(jnp.bfloat16))
        for head, out in enumerate(results):
            for k in range(outer):
                cut = slice(head * HEAD_DIM, (head + 1) * HEAD_DIM)
                outs[k][:, cut] = out[k * rows_here : (k + 1) * rows_here]

    return pl.pallas_call(
        body, out_shape=[jax.ShapeDtypeStruct((rows_here, share), jnp.bfloat16)] * outer,
        in_specs=[VMEM] * (1 + outer + len(pairs)), out_specs=[VMEM] * outer,
        name="attend_pieces",
    )(usable, *queries, *pairs)


def make_shards(parts):
    outer = math.gcd(4, parts // 2)
    inner = parts // outer
    same_outer = [[g * inner + i for i in range(inner)] for g in range(outer)]

    def send(piece, k):
        if k == 0:
            return piece
        return lax.ppermute(piece, "seq", [(s, s ^ (k * inner)) for s in range(parts)])

    def shards(queries, keys, values, bucket_lens, gate, out_weight):
        rows_here, width = queries.shape[1:]
        share = width // outer
        length = bucket_lens[0]
        here = lax.axis_index("seq")
        row, own = here // inner, here % inner
        position = here * rows_here + lax.iota(jnp.int32, rows_here)
        pairs, query = cut_pieces(row[None], queries[0], keys[0], values[0], outer)
        pairs = [send(p, k) for k, p in enumerate(pairs)]
        query = [send(p, k) for k, p in enumerate(query)]
        groups = row ^ lax.iota(jnp.int32, outer)
        if inner == 2:
            pairs = pairs + [
                lax.ppermute(p, "seq", [(s, s ^ 1) for s in range(parts)]) for p in pairs
            ]
            members = jnp.stack([own, 1 - own])
        else:
            pairs = [
                lax.all_gather(
                    jnp.concatenate(pairs, axis=0), "seq", axis=0, tiled=True,
                    axis_index_groups=same_outer,
                )
            ]
            members = lax.iota(jnp.int32, inner)
        places = (
            (groups[None, :, None] * inner + members[:, None, None]) * rows_here
            + lax.iota(jnp.int32, rows_here)[None, None, :]
        )
        usable = (places < length).astype(jnp.int32).reshape(1, -1)
        outs = attend_pieces(usable, query, pairs)
        back = [send(p, k) for k, p in enumerate(outs)]
        weight = jnp.concatenate(
            [lax.dynamic_slice_in_dim(out_weight, (row ^ k) * share, share, 0) for k in range(outer)], axis=0
        )
        attended = jnp.concatenate(back, axis=1)
        everyone = lax.all_gather(attended, "bucket", axis=0, tiled=True)
        projected = jnp.dot(everyone, weight, preferred_element_type=jnp.float32)
        projected = projected.astype(jnp.bfloat16).reshape(-1, rows_here, out_weight.shape[1])
        gathered = lax.all_to_all(projected, "bucket", split_axis=0, concat_axis=0, tiled=True)
        wide_rows = jnp.concatenate([gathered[c] for c in range(gathered.shape[0])], axis=1)
        result = wide_rows.astype(jnp.float32) * gate[0][None, :]
        return jnp.where((position < length)[:, None], result, 0.0).astype(jnp.bfloat16)[None]

    return shards


def solution(mesh):
    placed = (
        P("bucket", "seq", None),
        P("bucket", "seq", None),
        P("bucket", "seq", None),
        P("bucket"),
        P("bucket", None),
        P(None, "bucket"),
    )
    return jax.shard_map(
        make_shards(mesh.shape["seq"]),
        mesh=mesh, in_specs=placed, out_specs=P("bucket", "seq", None), check_vma=False,
    )
```

profile of v0, /device:TPU:0, one launch (start us, length us, event | category | flops | bytes accessed | tf_op | source)
XLA Modules:
  0.0 54.2 jit_solution(17487519228453383243)
XLA Ops:
  0.0 1.9 %cut_pieces.1 = (bf16[56,768]{1,0:T(8,128)(2,1)}, bf16[56,768]{1,0:T(8,128)(2,1)}, bf16[56,768]{1,0:T(8,128)(2,1)}, bf16[56,768]{1,0:T(8,128)(2,1)}, bf16[56,384...) custom-call(s32[1]{0:T(128)} %bitcast.3.row_ref, ...), custom_call_target="tpu_custom_call" | custom-call | tf_op jit(solution)/shard_map/cut_pieces/pallas_call | solution.py:31
  1.9 3.1 %collective-permute-start = (bf16[56,384]{1,0:T(8,128)(2,1)}, bf16[56,384]{1,0:T(8,128)(2,1)S(1)}, u32[]{:S(2)}, u32[]{:S(2)}) collective-permute-start(bf16[56,384]{1,0:T(8,128)(2,1)} %get-tuple-element.18), channel_id=1, source_target_pairs={{0,2},{1,3},{2,0},{3,1},{4,6},{5,7},{6,4},{7,5},{8,10},{9,11},{10,... | collective-permute-start | bytes 129032 | tf_op jit(solution)/shard_map/ppermute | solution.py:83
  5.0 2.6 %collective-permute-start.1 = (bf16[56,384]{1,0:T(8,128)(2,1)}, bf16[56,384]{1,0:T(8,128)(2,1)S(1)}, u32[]{:S(2)}, u32[]{:S(2)}) collective-permute-start(bf16[56,384]{1,0:T(8,128)(2,1)} %get-tuple-element.19), channel_id=1, source_target_pairs={{0,4},{1,5},{2,6},{3,7},{4,0},{5,1},{6,2},{7,3},{8,12},{9,13},{10,... | collective-permute-start | bytes 129032 | tf_op jit(solution)/shard_map/ppermute | solution.py:83
  7.5 0.4 collective-permute-start.3
  8.0 3.9 %collective-permute-start.5 = (bf16[56,768]{1,0:T(8,128)(2,1)}, bf16[56,768]{1,0:T(8,128)(2,1)S(1)}, u32[]{:S(2)}, u32[]{:S(2)}) collective-permute-start(bf16[56,768]{1,0:T(8,128)(2,1)} %get-tuple-element.24), channel_id=1, source_target_pairs={{0,6},{1,7},{2,4},{3,5},{4,2},{5,3},{6,0},{7,1},{8,14},{9,15},{10,... | collective-permute-start | bytes 258056 | tf_op jit(solution)/shard_map/ppermute | solution.py:83
  11.9 0.1 pad_add_fusion
  12.0 0.1 add_multiply_fusion
  12.8 0.1 collective-permute-start.2
  12.9 0.1 collective-permute-start.6
  13.0 0.5 collective-permute-start.7
  13.4 4.7 %collective-permute-done.4.refs_6_ = bf16[56,768]{1,0:T(8,128)(2,1)S(1)} collective-permute-done((bf16[56,768]{1,0:T(8,128)(2,1)}, bf16[56,768]{1,0:T(8,128)(2,1)S(1)}, u32[]{:S(2)}, u32[]{:S(2)}) %collective-permute-start.4) | collective-permute-done | bytes 86048 | tf_op jit(solution)/shard_map/ppermute | solution.py:83
  18.1 0.5 collective-permute-start.9
  18.6 0.1 fusion.11
  18.7 0.7 %reshape.182.usable_ref = s32[1,448]{1,0:T(1,128)} reshape(s32[2,4,56]{2,1,0:T(4,128)S(1)} %fusion.11) | data formatting | bytes 3584 | tf_op jit(solution)/shard_map/convert_element_type | solution.py:113
  19.4 0.1 collective-permute-done.9.refs_11_
  19.6 0.4 copy-done.10
  20.0 0.0 copy-done.3
  20.0 0.0 copy-done.4
  20.1 0.0 copy-done.5
  20.1 0.1 copy-done.6
  20.2 2.6 %attend_pieces.1 = (bf16[56,384]{1,0:T(8,128)(2,1)}, bf16[56,384]{1,0:T(8,128)(2,1)}, bf16[56,384]{1,0:T(8,128)(2,1)}, bf16[56,384]{1,0:T(8,128)(2,1)}) custom-call(s32[1,448]{1,0:T(1,128)} %reshape.182.usable_ref, bf16[56,384]{1,0:T(8,128)(2,1)} %get-tuple-element.17.refs_0_, bf16[56,384]{1,0:T(8,128)(2,1)} %copy-done.8, bf16[56,384]{1,0:T(8,128)(2,1)} %copy-done.9, ...), custom_call_target="tpu_custom_call" | custom-call | tf_op jit(solution)/shard_map/attend_pieces/pallas_call | solution.py:68
  22.8 1.8 %collective-permute-start.10 = (bf16[56,384]{1,0:T(8,128)(2,1)}, bf16[56,384]{1,0:T(8,128)(2,1)S(1)}, u32[]{:S(2)}, u32[]{:S(2)}) collective-permute-start(bf16[56,384]{1,0:T(8,128)(2,1)} %get-tuple-element.26), channel_id=1, source_target_pairs={{0,2},{1,3},{2,0},{3,1},{4,6},{5,7},{6,4},{7,5},{8,10},{9,11},{10,... | collective-permute-start | bytes 129032 | tf_op jit(solution)/shard_map/ppermute | solution.py:83
  24.6 0.9 %collective-permute-start.11 = (bf16[56,384]{1,0:T(8,128)(2,1)}, bf16[56,384]{1,0:T(8,128)(2,1)S(1)}, u32[]{:S(2)}, u32[]{:S(2)}) collective-permute-start(bf16[56,384]{1,0:T(8,128)(2,1)} %get-tuple-element.27), channel_id=1, source_target_pairs={{0,4},{1,5},{2,6},{3,7},{4,0},{5,1},{6,2},{7,3},{8,12},{9,13},{10,... | collective-permute-start | bytes 129032 | tf_op jit(solution)/shard_map/ppermute | solution.py:83
  25.5 1.6 %collective-permute-start.12 = (bf16[56,384]{1,0:T(8,128)(2,1)}, bf16[56,384]{1,0:T(8,128)(2,1)S(1)}, u32[]{:S(2)}, u32[]{:S(2)}) collective-permute-start(bf16[56,384]{1,0:T(8,128)(2,1)} %get-tuple-element.28), channel_id=1, source_target_pairs={{0,6},{1,7},{2,4},{3,5},{4,2},{5,3},{6,0},{7,1},{8,14},{9,15},{10,... | collective-permute-start | bytes 129032 | tf_op jit(solution)/shard_map/ppermute | solution.py:83
  27.2 1.8 %constant_dynamic-slice_fusion.3 = (bf16[384,768]{1,0:T(8,128)(2,1)S(1)}, bf16[384,768]{1,0:T(8,128)(2,1)S(1)}, bf16[384,768]{1,0:T(8,128)(2,1)S(1)}, bf16[384,768]{1,0:T(8,128)(2,1)S(1)}) fusion(bf16[1536,768]{1,0:T(8,128)(2,1)} %param.11, s32[]{:T(128)S(6)} %select_n.36, s32[]{:T(128)S(6)} %select_n.37, s32[]{:T(128)S(6)} %select_n.39, s32[]{:T(128)S(6)} %select_n.38), kind=kLoop, calls=%fused_computation.17 | loop fusion | bytes 4718608 | tf_op jit(solution)/shard_map/dynamic_slice | solution.py:117
  28.9 2.1 %collective-permute-done.11 = bf16[56,384]{1,0:T(8,128)(2,1)S(1)} collective-permute-done((bf16[56,384]{1,0:T(8,128)(2,1)}, bf16[56,384]{1,0:T(8,128)(2,1)S(1)}, u32[]{:S(2)}, u32[]{:S(2)}) %collective-permute-start.11) | collective-permute-done | bytes 43040 | tf_op jit(solution)/shard_map/ppermute | solution.py:83
  31.1 0.6 %collective-permute-done.12 = bf16[56,384]{1,0:T(8,128)(2,1)S(1)} collective-permute-done((bf16[56,384]{1,0:T(8,128)(2,1)}, bf16[56,384]{1,0:T(8,128)(2,1)S(1)}, u32[]{:S(2)}, u32[]{:S(2)}) %collective-permute-start.12) | collective-permute-done | bytes 43040 | tf_op jit(solution)/shard_map/ppermute | solution.py:83
  31.7 10.9 %all_gather.3 = bf16[224,1536]{1,0:T(8,128)(2,1)S(1)} all-gather(bf16[56,1536]{1,0:T(8,128)(2,1)S(1)} %pad_maximum_fusion), channel_id=1, replica_groups=mesh['bucket'=4,'seq'=8] {'bucket'}, dimensions={0}, use_global_device_ids=true | all-gather | bytes 860160 | tf_op jit(solution)/shard_map/all_gather | solution.py:120
  42.6 1.4 %fusion.8 = bf16[224,768]{1,0:T(8,128)(2,1)} fusion(bf16[224,1536]{1,0:T(8,128)(2,1)S(1)} %all_gather.3, bf16[384,768]{1,0:T(8,128)(2,1)S(1)} %get-tuple-element.31, bf16[384,768]{1,0:T(8,128)(2,1)S(1)} %get-tuple-element.32, bf16[384,768]{1,0:T(8,128)(2,1)S(1)} %get-tuple-element.30, bf16[384,768]{1,0:T(8,128)(2,1)S(1)} %get-tuple-element.29), kind=kOutput, calls=%fused_computation.8 | convolution fusion | flops 538091520 | bytes 3391488 | tf_op jit(solution)/shard_map/dot_general | solution.py:121
  44.0 3.5 %all-to-all-start = ((bf16[4,56,768]{2,1,0:T(8,128)(2,1)}), bf16[4,56,768]{2,1,0:T(8,128)(2,1)S(1)}, u32[]{:S(2)}, u32[]{:S(2)}) async-start(bf16[4,56,768]{2,1,0:T(8,128)(2,1)} %bitcast.7), calls=%async_computation | async-start | bytes 688128 | tf_op jit(solution)/shard_map/all_to_all | solution.py:123
  47.5 5.8 %all-to-all-done = bf16[4,56,768]{2,1,0:T(8,128)(2,1)S(1)} async-done(((bf16[4,56,768]{2,1,0:T(8,128)(2,1)}), bf16[4,56,768]{2,1,0:T(8,128)(2,1)S(1)}, u32[]{:S(2)}, u32[]{:S(2)}) %all-to-all-start) | async-done | bytes 344096 | tf_op jit(solution)/shard_map/all_to_all | solution.py:123
  53.3 0.8 %select_convert_fusion = bf16[1,56,3072]{2,1,0:T(8,128)(2,1)} fusion(bf16[1,56,768]{2,1,0:T(8,128)(2,1)S(1)} %get-tuple-element.34, bf16[1,56,768]{2,1,0:T(8,128)(2,1)S(1)} %get-tuple-element.35, bf16[1,56,768]{2,1,0:T(8,128)(2,1)S(1)} %get-tuple-element.36, bf16[1,56,768]{2,1,0:T(8,128)(2,1)S(1)} %get-tuple-element.33, f32[3072]{0:T(1024)S(1)} %bitcast.15, ...), kind=kLoop, calls=%fused_computation.9 | loop fusion | flops 1892352 | bytes 700472 | tf_op jit(solution)/shard_map/convert_element_type | solution.py:126
  (34 shorter events, 0.1 us)
Async XLA Ops:
  1.9 10.8 %collective-permute-start = (bf16[56,384]{1,0:T(8,128)(2,1)}, bf16[56,384]{1,0:T(8,128)(2,1)S(1)}, u32[]{:S(2)}, u32[]{:S(2)}) collective-permute-start(bf16[56,384]{1,0:T(8,128)(2,1)} %get-tuple-element.18), channel_id=1, source_target_pairs={{0,2},{1,3},{2,0},{3,1},{4,6},{5,7},{6,4},{7,5},{8,10},{9,11},{10,... | collective-permute-start | bytes 129032 | tf_op jit(solution)/shard_map/ppermute | solution.py:83
  5.0 7.9 %collective-permute-start.1 = (bf16[56,384]{1,0:T(8,128)(2,1)}, bf16[56,384]{1,0:T(8,128)(2,1)S(1)}, u32[]{:S(2)}, u32[]{:S(2)}) collective-permute-start(bf16[56,384]{1,0:T(8,128)(2,1)} %get-tuple-element.19), channel_id=1, source_target_pairs={{0,4},{1,5},{2,6},{3,7},{4,0},{5,1},{6,2},{7,3},{8,12},{9,13},{10,... | collective-permute-start | bytes 129032 | tf_op jit(solution)/shard_map/ppermute | solution.py:83
  7.5 5.4 %collective-permute-start.3 = (bf16[56,768]{1,0:T(8,128)(2,1)}, bf16[56,768]{1,0:T(8,128)(2,1)S(1)}, u32[]{:S(2)}, u32[]{:S(2)}) collective-permute-start(bf16[56,768]{1,0:T(8,128)(2,1)} %get-tuple-element.22), channel_id=1, source_target_pairs={{0,2},{1,3},{2,0},{3,1},{4,6},{5,7},{6,4},{7,5},{8,10},{9,11},{10,... | collective-permute-start | bytes 258056 | tf_op jit(solution)/shard_map/ppermute | solution.py:83
  8.0 10.1 %collective-permute-start.4 = (bf16[56,768]{1,0:T(8,128)(2,1)}, bf16[56,768]{1,0:T(8,128)(2,1)S(1)}, u32[]{:S(2)}, u32[]{:S(2)}) collective-permute-start(bf16[56,768]{1,0:T(8,128)(2,1)} %get-tuple-element.23), channel_id=1, source_target_pairs={{0,4},{1,5},{2,6},{3,7},{4,0},{5,1},{6,2},{7,3},{8,12},{9,13},{10,... | collective-permute-start | bytes 258056 | tf_op jit(solution)/shard_map/ppermute | solution.py:83
  8.0 10.1 %collective-permute-start.5 = (bf16[56,768]{1,0:T(8,128)(2,1)}, bf16[56,768]{1,0:T(8,128)(2,1)S(1)}, u32[]{:S(2)}, u32[]{:S(2)}) collective-permute-start(bf16[56,768]{1,0:T(8,128)(2,1)} %get-tuple-element.24), channel_id=1, source_target_pairs={{0,6},{1,7},{2,4},{3,5},{4,2},{5,3},{6,0},{7,1},{8,14},{9,15},{10,... | collective-permute-start | bytes 258056 | tf_op jit(solution)/shard_map/ppermute | solution.py:83
  12.7 6.8 %copy-start.8 = (bf16[56,384]{1,0:T(8,128)(2,1)}, bf16[56,384]{1,0:T(8,128)(2,1)S(1)}, u32[]{:S(2)}) copy-start(bf16[56,384]{1,0:T(8,128)(2,1)S(1)} %collective-permute-done.refs_1_) | copy-start | bytes 129028
  12.8 6.6 %collective-permute-start.2 = (bf16[56,384]{1,0:T(8,128)(2,1)}, bf16[56,384]{1,0:T(8,128)(2,1)S(1)}, u32[]{:S(2)}, u32[]{:S(2)}) collective-permute-start(bf16[56,384]{1,0:T(8,128)(2,1)} %get-tuple-element.20), channel_id=1, source_target_pairs={{0,6},{1,7},{2,4},{3,5},{4,2},{5,3},{6,0},{7,1},{8,14},{9,15},{10,... | collective-permute-start | bytes 129032 | tf_op jit(solution)/shard_map/ppermute | solution.py:83
  12.8 6.7 %copy-start.9 = (bf16[56,384]{1,0:T(8,128)(2,1)}, bf16[56,384]{1,0:T(8,128)(2,1)S(1)}, u32[]{:S(2)}) copy-start(bf16[56,384]{1,0:T(8,128)(2,1)S(1)} %collective-permute-done.1.refs_2_) | copy-start | bytes 129028
  12.9 6.5 %collective-permute-start.6 = (bf16[56,768]{1,0:T(8,128)(2,1)}, bf16[56,768]{1,0:T(8,128)(2,1)S(1)}, u32[]{:S(2)}, u32[]{:S(2)}) collective-permute-start(bf16[56,768]{1,0:T(8,128)(2,1)} %get-tuple-element.21.refs_4_), channel_id=1, source_target_pairs={{0,1},{1,0},{2,3},{3,2},{4,5},{5,4},{6,7},{7,6},{8,9},{9,8},{10,11... | collective-permute-start | bytes 258056 | tf_op jit(solution)/shard_map/ppermute | solution.py:98
  12.9 6.6 %copy-start = (bf16[56,768]{1,0:T(8,128)(2,1)}, bf16[56,768]{1,0:T(8,128)(2,1)S(1)}, u32[]{:S(2)}) copy-start(bf16[56,768]{1,0:T(8,128)(2,1)S(1)} %collective-permute-done.3.refs_5_) | copy-start | bytes 258052
  13.0 6.4 %collective-permute-start.7 = (bf16[56,768]{1,0:T(8,128)(2,1)S(1)}, bf16[56,768]{1,0:T(8,128)(2,1)S(1)}, u32[]{:S(2)}, u32[]{:S(2)}) collective-permute-start(bf16[56,768]{1,0:T(8,128)(2,1)S(1)} %collective-permute-done.3.refs_5_), channel_id=1, source_target_pairs={{0,1},{1,0},{2,3},{3,2},{4,5},{5,4},{6,7},{7,6},{8,9},{9,8},{10,11... | collective-permute-start | bytes 258056 | tf_op jit(solution)/shard_map/ppermute | solution.py:98
  18.1 1.5 %copy-start.1 = (bf16[56,768]{1,0:T(8,128)(2,1)}, bf16[56,768]{1,0:T(8,128)(2,1)S(1)}, u32[]{:S(2)}) copy-start(bf16[56,768]{1,0:T(8,128)(2,1)S(1)} %collective-permute-done.4.refs_6_) | copy-start | bytes 258052
  18.1 1.3 %collective-permute-start.8 = (bf16[56,768]{1,0:T(8,128)(2,1)S(1)}, bf16[56,768]{1,0:T(8,128)(2,1)S(1)}, u32[]{:S(2)}, u32[]{:S(2)}) collective-permute-start(bf16[56,768]{1,0:T(8,128)(2,1)S(1)} %collective-permute-done.4.refs_6_), channel_id=1, source_target_pairs={{0,1},{1,0},{2,3},{3,2},{4,5},{5,4},{6,7},{7,6},{8,9},{9,8},{10,11... | collective-permute-start | bytes 258056 | tf_op jit(solution)/shard_map/ppermute | solution.py:98
  18.1 1.5 %copy-start.2 = (bf16[56,768]{1,0:T(8,128)(2,1)}, bf16[56,768]{1,0:T(8,128)(2,1)S(1)}, u32[]{:S(2)}) copy-start(bf16[56,768]{1,0:T(8,128)(2,1)S(1)} %collective-permute-done.5.refs_7_) | copy-start | bytes 258052
  18.1 1.4 %collective-permute-start.9 = (bf16[56,768]{1,0:T(8,128)(2,1)S(1)}, bf16[56,768]{1,0:T(8,128)(2,1)S(1)}, u32[]{:S(2)}, u32[]{:S(2)}) collective-permute-start(bf16[56,768]{1,0:T(8,128)(2,1)S(1)} %collective-permute-done.5.refs_7_), channel_id=1, source_target_pairs={{0,1},{1,0},{2,3},{3,2},{4,5},{5,4},{6,7},{7,6},{8,9},{9,8},{10,11... | collective-permute-start | bytes 258056 | tf_op jit(solution)/shard_map/ppermute | solution.py:98
  19.4 0.6 %copy-start.10 = (bf16[56,384]{1,0:T(8,128)(2,1)}, bf16[56,384]{1,0:T(8,128)(2,1)S(1)}, u32[]{:S(2)}) copy-start(bf16[56,384]{1,0:T(8,128)(2,1)S(1)} %collective-permute-done.2.refs_3_) | copy-start | bytes 129028
  19.4 0.6 %copy-start.3 = (bf16[56,768]{1,0:T(8,128)(2,1)}, bf16[56,768]{1,0:T(8,128)(2,1)S(1)}, u32[]{:S(2)}) copy-start(bf16[56,768]{1,0:T(8,128)(2,1)S(1)} %collective-permute-done.6.refs_8_) | copy-start | bytes 258052
  19.4 0.7 %copy-start.4 = (bf16[56,768]{1,0:T(8,128)(2,1)}, bf16[56,768]{1,0:T(8,128)(2,1)S(1)}, u32[]{:S(2)}) copy-start(bf16[56,768]{1,0:T(8,128)(2,1)S(1)} %collective-permute-done.7.refs_9_) | copy-start | bytes 258052
  19.4 0.7 %copy-start.5 = (bf16[56,768]{1,0:T(8,128)(2,1)}, bf16[56,768]{1,0:T(8,128)(2,1)S(1)}, u32[]{:S(2)}) copy-start(bf16[56,768]{1,0:T(8,128)(2,1)S(1)} %collective-permute-done.8.refs_10_) | copy-start | bytes 258052
  19.5 0.6 %copy-start.6 = (bf16[56,768]{1,0:T(8,128)(2,1)}, bf16[56,768]{1,0:T(8,128)(2,1)S(1)}, u32[]{:S(2)}) copy-start(bf16[56,768]{1,0:T(8,128)(2,1)S(1)} %collective-permute-done.9.refs_11_) | copy-start | bytes 258052
  22.8 6.1 %collective-permute-start.10 = (bf16[56,384]{1,0:T(8,128)(2,1)}, bf16[56,384]{1,0:T(8,128)(2,1)S(1)}, u32[]{:S(2)}, u32[]{:S(2)}) collective-permute-start(bf16[56,384]{1,0:T(8,128)(2,1)} %get-tuple-element.26), channel_id=1, source_target_pairs={{0,2},{1,3},{2,0},{3,1},{4,6},{5,7},{6,4},{7,5},{8,10},{9,11},{10,... | collective-permute-start | bytes 129032 | tf_op jit(solution)/shard_map/ppermute | solution.py:83
  24.6 6.5 %collective-permute-start.11 = (bf16[56,384]{1,0:T(8,128)(2,1)}, bf16[56,384]{1,0:T(8,128)(2,1)S(1)}, u32[]{:S(2)}, u32[]{:S(2)}) collective-permute-start(bf16[56,384]{1,0:T(8,128)(2,1)} %get-tuple-element.27), channel_id=1, source_target_pairs={{0,4},{1,5},{2,6},{3,7},{4,0},{5,1},{6,2},{7,3},{8,12},{9,13},{10,... | collective-permute-start | bytes 129032 | tf_op jit(solution)/shard_map/ppermute | solution.py:83
  25.5 6.1 %copy-start.7 = (bf16[56,384]{1,0:T(8,128)(2,1)S(1)}, bf16[56,384]{1,0:T(8,128)(2,1)}, u32[]{:S(2)}) copy-start(bf16[56,384]{1,0:T(8,128)(2,1)} %get-tuple-element.25) | copy-start | bytes 129028
  25.5 6.1 %collective-permute-start.12 = (bf16[56,384]{1,0:T(8,128)(2,1)}, bf16[56,384]{1,0:T(8,128)(2,1)S(1)}, u32[]{:S(2)}, u32[]{:S(2)}) collective-permute-start(bf16[56,384]{1,0:T(8,128)(2,1)} %get-tuple-element.28), channel_id=1, source_target_pairs={{0,6},{1,7},{2,4},{3,5},{4,2},{5,3},{6,0},{7,1},{8,14},{9,15},{10,... | collective-permute-start | bytes 129032 | tf_op jit(solution)/shard_map/ppermute | solution.py:83
  42.6 10.7 %copy-start.11 = (f32[1,3072]{1,0:T(1,128)S(1)}, f32[1,3072]{1,0:T(1,128)}, u32[]{:S(2)}) copy-start(f32[1,3072]{1,0:T(1,128)} %param.10) | copy-start | bytes 36868
  44.0 9.3 %all-to-all-start = ((bf16[4,56,768]{2,1,0:T(8,128)(2,1)}), bf16[4,56,768]{2,1,0:T(8,128)(2,1)S(1)}, u32[]{:S(2)}, u32[]{:S(2)}) async-start(bf16[4,56,768]{2,1,0:T(8,128)(2,1)} %bitcast.7), calls=%async_computation | async-start | bytes 688128 | tf_op jit(solution)/shard_map/all_to_all | solution.py:123
where the time goes:
time: 54.5 us; the launch traced here: 54.2 us
  starting transfers between devices  19 us (35%)
  waiting for transfers between devices  13.3 us (24%)
  blocking collectives  10.9 us (20%)
  Pallas kernels  4.51 us (8%)
  local copies, waits for them, and re-layouts  3.07 us (6%)
  matrix products  1.43 us (3%)
  other arithmetic  1.09 us (2%)
  between operations  0.84 us (2%)
    ppermute x9, starting transfers between devices, send(): lax.ppermute(piece, 'seq', [(s, s ^ k * inner) for s in range(parts)])  14.5 us
    all_gather x1, blocking collectives, shards(): everyone = lax.all_gather(attended, 'bucket', axis=0, tiled=True)  10.9 us
    ppermute x9, waiting for transfers between devices, send(): lax.ppermute(piece, 'seq', [(s, s ^ k * inner) for s in range(parts)])  7.41 us
    all_to_all x1, waiting for transfers between devices, shards(): lax.all_to_all(projected, 'bucket', split_axis=0, concat_axis=0, tiled=True)  5.76 us
    all_to_all x1, starting transfers between devices, shards(): lax.all_to_all(projected, 'bucket', split_axis=0, concat_axis=0, tiled=True)  3.49 us
    pallas_call x1, Pallas kernels, attend_pieces(): pl.pallas_call(body, out_shape=[jax.ShapeDtypeStruct((rows_here, share),...  2.61 us
    pallas_call x1, Pallas kernels, cut_pieces(): pl.pallas_call(body, out_shape=shapes, in_specs=[SMEM, VMEM, VMEM, VMEM],...  1.9 us
    dynamic_slice x1, local copies, waits for them, and re-layouts, shards(): lax.dynamic_slice_in_dim(out_weight, (row ^ k) * share, share, 0)  1.75 us
  transfers between devices with their start and end apart: 14, of which 5 were waited for; matrix products, arithmetic and copies ran while one was open for 5% of the time, Pallas kernels for 0%

commit v1 on v0

--- a/solution.py
+++ b/solution.py
@@ -15,24 +15,22 @@
 SMEM = pl.BlockSpec(memory_space=pltpu.SMEM)
 
 
-def cut_pieces(row, queries, keys, values, outer):
-    rows, width = queries.shape
+def cut_pieces(row, arrays, outer):
+    rows, width = arrays[0].shape
     share = width // outer
 
-    def body(row_ref, q_ref, k_ref, v_ref, *outs):
+    def body(row_ref, *refs):
         for k in range(outer):
             cut = pl.ds(pl.multiple_of((row_ref[0] ^ k) * share, HEAD_DIM), share)
-            outs[k][:, :share] = k_ref[:, cut]
-            outs[k][:, share:] = v_ref[:, cut]
-            outs[outer + k][...] = q_ref[:, cut]
+            for which in range(len(arrays)):
+                place = slice(which * share, (which + 1) * share)
+                refs[len(arrays) + k][:, place] = refs[which][:, cut]
 
-    shapes = [jax.ShapeDtypeStruct((rows, 2 * share), queries.dtype)] * outer
-    shapes += [jax.ShapeDtypeStruct((rows, share), queries.dtype)] * outer
-    out = pl.pallas_call(
-        body, out_shape=shapes, in_specs=[SMEM, VMEM, VMEM, VMEM], out_specs=[VMEM] * (2 * outer),
-        name="cut_pieces",
-    )(row, queries, keys, values)
-    return out[:outer], out[outer:]
+    shape = jax.ShapeDtypeStruct((rows, len(arrays) * share), arrays[0].dtype)
+    return pl.pallas_call(
+        body, out_shape=[shape] * outer, in_specs=[SMEM] + [VMEM] * len(arrays),
+        out_specs=[VMEM] * outer, name="cut_pieces",
+    )(row, *arrays)
 
 
 def attend_pieces(usable, queries, pairs):
@@ -89,7 +87,8 @@
         here = lax.axis_index("seq")
         row, own = here // inner, here % inner
         position = here * rows_here + lax.iota(jnp.int32, rows_here)
-        pairs, query = cut_pieces(row[None], queries[0], keys[0], values[0], outer)
+        pairs = cut_pieces(row[None], [keys[0], values[0]], outer)
+        query = cut_pieces(row[None], [queries[0]], outer)
         pairs = [send(p, k) for k, p in enumerate(pairs)]
         query = [send(p, k) for k, p in enumerate(query)]
         groups = row ^ lax.iota(jnp.int32, outer)

time: 54.5 us -> 55.4 us (1.017)
  Pallas kernels: 4.51 us -> 5.96 us
    pallas_call x1 -> x2, Pallas kernels: 1.9 us -> 3.37 us  [cut_pieces(): pl.pallas_call(body, out_shape=[shape] * outer, in_specs=[SMEM] + [VMEM]...]
  transfers between devices with their start and end apart: 14 -> 14, of which waited for: 5 -> 4; matrix products, arithmetic and copies ran while one was open for 5% -> 5% of each run, Pallas kernels for 0% -> 3%
where the time goes in v1:
time: 55.4 us; the launch traced here: 55.1 us
  starting transfers between devices  19.2 us (35%)
  waiting for transfers between devices  12.8 us (23%)
  blocking collectives  10.7 us (19%)
  Pallas kernels  5.96 us (11%)
  local copies, waits for them, and re-layouts  3.06 us (6%)
  matrix products  1.43 us (3%)
  other arithmetic  1.09 us (2%)
  between operations  0.84 us (2%)
    ppermute x9, starting transfers between devices, send(): lax.ppermute(piece, 'seq', [(s, s ^ k * inner) for s in range(parts)])  14.5 us
    all_gather x1, blocking collectives, shards(): everyone = lax.all_gather(attended, 'bucket', axis=0, tiled=True)  10.7 us
    ppermute x9, waiting for transfers between devices, send(): lax.ppermute(piece, 'seq', [(s, s ^ k * inner) for s in range(parts)])  6.92 us
    all_to_all x1, waiting for transfers between devices, shards(): lax.all_to_all(projected, 'bucket', split_axis=0, concat_axis=0, tiled=True)  5.76 us
    all_to_all x1, starting transfers between devices, shards(): lax.all_to_all(projected, 'bucket', split_axis=0, concat_axis=0, tiled=True)  3.62 us
    pallas_call x2, Pallas kernels, cut_pieces(): pl.pallas_call(body, out_shape=[shape] * outer, in_specs=[SMEM] + [VMEM]...  3.37 us
    pallas_call x1, Pallas kernels, attend_pieces(): pl.pallas_call(body, out_shape=[jax.ShapeDtypeStruct((rows_here, share),...  2.59 us
    dynamic_slice x1, local copies, waits for them, and re-layouts, shards(): lax.dynamic_slice_in_dim(out_weight, (row ^ k) * share, share, 0)  1.75 us
  transfers between devices with their start and end apart: 14, of which 4 were waited for; matrix products, arithmetic and copies ran while one was open for 5% of the time, Pallas kernels for 3%

profile of v1, /device:TPU:0, one launch (start us, length us, event | category | flops | bytes accessed | tf_op | source)
XLA Modules:
  0.0 55.1 jit_solution(16451971004542242545)
XLA Ops:
  0.0 1.6 %cut_pieces.2 = (bf16[56,384]{1,0:T(8,128)(2,1)}, bf16[56,384]{1,0:T(8,128)(2,1)}, bf16[56,384]{1,0:T(8,128)(2,1)}, bf16[56,384]{1,0:T(8,128)(2,1)}) custom-call(s32[1]{0:T(128)} %bitcast.3.row_ref, bf16[56,1536]{1,0:T(8,128)(2,1)} %bitcast.14), custom_call_target="tpu_custom_call" | custom-call | tf_op jit(solution)/shard_map/cut_pieces/pallas_call | solution.py:30
  1.6 3.1 %collective-permute-start = (bf16[56,384]{1,0:T(8,128)(2,1)}, bf16[56,384]{1,0:T(8,128)(2,1)S(1)}, u32[]{:S(2)}, u32[]{:S(2)}) collective-permute-start(bf16[56,384]{1,0:T(8,128)(2,1)} %get-tuple-element.18), channel_id=1, source_target_pairs={{0,2},{1,3},{2,0},{3,1},{4,6},{5,7},{6,4},{7,5},{8,10},{9,11},{10,... | collective-permute-start | bytes 129032 | tf_op jit(solution)/shard_map/ppermute | solution.py:81
  4.7 2.6 %collective-permute-start.1 = (bf16[56,384]{1,0:T(8,128)(2,1)}, bf16[56,384]{1,0:T(8,128)(2,1)S(1)}, u32[]{:S(2)}, u32[]{:S(2)}) collective-permute-start(bf16[56,384]{1,0:T(8,128)(2,1)} %get-tuple-element.19), channel_id=1, source_target_pairs={{0,4},{1,5},{2,6},{3,7},{4,0},{5,1},{6,2},{7,3},{8,12},{9,13},{10,... | collective-permute-start | bytes 129032 | tf_op jit(solution)/shard_map/ppermute | solution.py:81
  7.3 1.7 %cut_pieces.3 = (bf16[56,768]{1,0:T(8,128)(2,1)}, bf16[56,768]{1,0:T(8,128)(2,1)}, bf16[56,768]{1,0:T(8,128)(2,1)}, bf16[56,768]{1,0:T(8,128)(2,1)}) custom-call(s32[1]{0:T(128)} %bitcast.3.row_ref, bf16[56,1536]{1,0:T(8,128)(2,1)} %bitcast.12, bf16[56,1536]{1,0:T(8,128)(2,1)} %bitcast.13), custom_call_target="tpu_custom_call" | custom-call | tf_op jit(solution)/shard_map/cut_pieces/pallas_call | solution.py:30
  9.0 0.4 collective-permute-start.3
  9.5 3.9 %collective-permute-start.5 = (bf16[56,768]{1,0:T(8,128)(2,1)}, bf16[56,768]{1,0:T(8,128)(2,1)S(1)}, u32[]{:S(2)}, u32[]{:S(2)}) collective-permute-start(bf16[56,768]{1,0:T(8,128)(2,1)} %get-tuple-element.24), channel_id=1, source_target_pairs={{0,6},{1,7},{2,4},{3,5},{4,2},{5,3},{6,0},{7,1},{8,14},{9,15},{10,... | collective-permute-start | bytes 258056 | tf_op jit(solution)/shard_map/ppermute | solution.py:81
  13.4 0.1 pad_add_fusion
  13.5 0.1 add_multiply_fusion
  14.2 0.1 collective-permute-start.2
  14.3 0.1 collective-permute-start.6
  14.4 0.5 collective-permute-start.7
  14.9 4.6 %collective-permute-done.4.refs_6_ = bf16[56,768]{1,0:T(8,128)(2,1)S(1)} collective-permute-done((bf16[56,768]{1,0:T(8,128)(2,1)}, bf16[56,768]{1,0:T(8,128)(2,1)S(1)}, u32[]{:S(2)}, u32[]{:S(2)}) %collective-permute-start.4) | collective-permute-done | bytes 86048 | tf_op jit(solution)/shard_map/ppermute | solution.py:81
  19.6 0.5 collective-permute-start.9
  20.1 0.1 fusion.11
  20.1 0.7 %reshape.182.usable_ref = s32[1,448]{1,0:T(1,128)} reshape(s32[2,4,56]{2,1,0:T(4,128)S(1)} %fusion.11) | data formatting | bytes 3584 | tf_op jit(solution)/shard_map/convert_element_type | solution.py:112
  20.8 0.1 collective-permute-done.9.refs_11_
  21.0 0.4 copy-done.10
  21.4 0.1 copy-done.3
  21.4 0.0 copy-done.4
  21.5 0.0 copy-done.5
  21.5 0.1 copy-done.6
  21.6 2.6 %attend_pieces.1 = (bf16[56,384]{1,0:T(8,128)(2,1)}, bf16[56,384]{1,0:T(8,128)(2,1)}, bf16[56,384]{1,0:T(8,128)(2,1)}, bf16[56,384]{1,0:T(8,128)(2,1)}) custom-call(s32[1,448]{1,0:T(1,128)} %reshape.182.usable_ref, bf16[56,384]{1,0:T(8,128)(2,1)} %get-tuple-element.17.refs_0_, bf16[56,384]{1,0:T(8,128)(2,1)} %copy-done.8, bf16[56,384]{1,0:T(8,128)(2,1)} %copy-done.9, ...), custom_call_target="tpu_custom_call" | custom-call | tf_op jit(solution)/shard_map/attend_pieces/pallas_call | solution.py:66
  24.2 1.8 %collective-permute-start.10 = (bf16[56,384]{1,0:T(8,128)(2,1)}, bf16[56,384]{1,0:T(8,128)(2,1)S(1)}, u32[]{:S(2)}, u32[]{:S(2)}) collective-permute-start(bf16[56,384]{1,0:T(8,128)(2,1)} %get-tuple-element.26), channel_id=1, source_target_pairs={{0,2},{1,3},{2,0},{3,1},{4,6},{5,7},{6,4},{7,5},{8,10},{9,11},{10,... | collective-permute-start | bytes 129032 | tf_op jit(solution)/shard_map/ppermute | solution.py:81
  26.0 0.3 collective-permute-start.11
  26.2 2.3 %collective-permute-start.12 = (bf16[56,384]{1,0:T(8,128)(2,1)}, bf16[56,384]{1,0:T(8,128)(2,1)S(1)}, u32[]{:S(2)}, u32[]{:S(2)}) collective-permute-start(bf16[56,384]{1,0:T(8,128)(2,1)} %get-tuple-element.28), channel_id=1, source_target_pairs={{0,6},{1,7},{2,4},{3,5},{4,2},{5,3},{6,0},{7,1},{8,14},{9,15},{10,... | collective-permute-start | bytes 129032 | tf_op jit(solution)/shard_map/ppermute | solution.py:81
  28.6 1.8 %constant_dynamic-slice_fusion.3 = (bf16[384,768]{1,0:T(8,128)(2,1)S(1)}, bf16[384,768]{1,0:T(8,128)(2,1)S(1)}, bf16[384,768]{1,0:T(8,128)(2,1)S(1)}, bf16[384,768]{1,0:T(8,128)(2,1)S(1)}) fusion(bf16[1536,768]{1,0:T(8,128)(2,1)} %param.11, s32[]{:T(128)S(6)} %select_n.36, s32[]{:T(128)S(6)} %select_n.37, s32[]{:T(128)S(6)} %select_n.39, s32[]{:T(128)S(6)} %select_n.38), kind=kLoop, calls=%fused_computation.17 | loop fusion | bytes 4718608 | tf_op jit(solution)/shard_map/dynamic_slice | solution.py:116
  30.4 2.3 %collective-permute-done.11 = bf16[56,384]{1,0:T(8,128)(2,1)S(1)} collective-permute-done((bf16[56,384]{1,0:T(8,128)(2,1)}, bf16[56,384]{1,0:T(8,128)(2,1)S(1)}, u32[]{:S(2)}, u32[]{:S(2)}) %collective-permute-start.11) | collective-permute-done | bytes 43040 | tf_op jit(solution)/shard_map/ppermute | solution.py:81
  32.7 10.7 %all_gather.3 = bf16[224,1536]{1,0:T(8,128)(2,1)S(1)} all-gather(bf16[56,1536]{1,0:T(8,128)(2,1)S(1)} %pad_maximum_fusion), channel_id=1, replica_groups=mesh['bucket'=4,'seq'=8] {'bucket'}, dimensions={0}, use_global_device_ids=true | all-gather | bytes 860160 | tf_op jit(solution)/shard_map/all_gather | solution.py:119
  43.4 1.4 %fusion.8 = bf16[224,768]{1,0:T(8,128)(2,1)} fusion(bf16[224,1536]{1,0:T(8,128)(2,1)S(1)} %all_gather.3, bf16[384,768]{1,0:T(8,128)(2,1)S(1)} %get-tuple-element.31, bf16[384,768]{1,0:T(8,128)(2,1)S(1)} %get-tuple-element.32, bf16[384,768]{1,0:T(8,128)(2,1)S(1)} %get-tuple-element.30, bf16[384,768]{1,0:T(8,128)(2,1)S(1)} %get-tuple-element.29), kind=kOutput, calls=%fused_computation.8 | convolution fusion | flops 538091520 | bytes 3391488 | tf_op jit(solution)/shard_map/dot_general | solution.py:120
  44.8 3.6 %all-to-all-start = ((bf16[4,56,768]{2,1,0:T(8,128)(2,1)}), bf16[4,56,768]{2,1,0:T(8,128)(2,1)S(1)}, u32[]{:S(2)}, u32[]{:S(2)}) async-start(bf16[4,56,768]{2,1,0:T(8,128)(2,1)} %bitcast.7), calls=%async_computation | async-start | bytes 688128 | tf_op jit(solution)/shard_map/all_to_all | solution.py:122
  48.4 5.8 %all-to-all-done = bf16[4,56,768]{2,1,0:T(8,128)(2,1)S(1)} async-done(((bf16[4,56,768]{2,1,0:T(8,128)(2,1)}), bf16[4,56,768]{2,1,0:T(8,128)(2,1)S(1)}, u32[]{:S(2)}, u32[]{:S(2)}) %all-to-all-start) | async-done | bytes 344096 | tf_op jit(solution)/shard_map/all_to_all | solution.py:122
  54.2 0.8 %select_convert_fusion = bf16[1,56,3072]{2,1,0:T(8,128)(2,1)} fusion(bf16[1,56,768]{2,1,0:T(8,128)(2,1)S(1)} %get-tuple-element.34, bf16[1,56,768]{2,1,0:T(8,128)(2,1)S(1)} %get-tuple-element.35, bf16[1,56,768]{2,1,0:T(8,128)(2,1)S(1)} %get-tuple-element.36, bf16[1,56,768]{2,1,0:T(8,128)(2,1)S(1)} %get-tuple-element.33, f32[3072]{0:T(1024)S(1)} %bitcast.15, ...), kind=kLoop, calls=%fused_computation.9 | loop fusion | flops 1892352 | bytes 700472 | tf_op jit(solution)/shard_map/convert_element_type | solution.py:125
  (35 shorter events, 0.1 us)
Async XLA Ops:
  1.6 12.6 %collective-permute-start = (bf16[56,384]{1,0:T(8,128)(2,1)}, bf16[56,384]{1,0:T(8,128)(2,1)S(1)}, u32[]{:S(2)}, u32[]{:S(2)}) collective-permute-start(bf16[56,384]{1,0:T(8,128)(2,1)} %get-tuple-element.18), channel_id=1, source_target_pairs={{0,2},{1,3},{2,0},{3,1},{4,6},{5,7},{6,4},{7,5},{8,10},{9,11},{10,... | collective-permute-start | bytes 129032 | tf_op jit(solution)/shard_map/ppermute | solution.py:81
  4.7 9.6 %collective-permute-start.1 = (bf16[56,384]{1,0:T(8,128)(2,1)}, bf16[56,384]{1,0:T(8,128)(2,1)S(1)}, u32[]{:S(2)}, u32[]{:S(2)}) collective-permute-start(bf16[56,384]{1,0:T(8,128)(2,1)} %get-tuple-element.19), channel_id=1, source_target_pairs={{0,4},{1,5},{2,6},{3,7},{4,0},{5,1},{6,2},{7,3},{8,12},{9,13},{10,... | collective-permute-start | bytes 129032 | tf_op jit(solution)/shard_map/ppermute | solution.py:81
  9.0 5.4 %collective-permute-start.3 = (bf16[56,768]{1,0:T(8,128)(2,1)}, bf16[56,768]{1,0:T(8,128)(2,1)S(1)}, u32[]{:S(2)}, u32[]{:S(2)}) collective-permute-start(bf16[56,768]{1,0:T(8,128)(2,1)} %get-tuple-element.22), channel_id=1, source_target_pairs={{0,2},{1,3},{2,0},{3,1},{4,6},{5,7},{6,4},{7,5},{8,10},{9,11},{10,... | collective-permute-start | bytes 258056 | tf_op jit(solution)/shard_map/ppermute | solution.py:81
  9.5 10.1 %collective-permute-start.4 = (bf16[56,768]{1,0:T(8,128)(2,1)}, bf16[56,768]{1,0:T(8,128)(2,1)S(1)}, u32[]{:S(2)}, u32[]{:S(2)}) collective-permute-start(bf16[56,768]{1,0:T(8,128)(2,1)} %get-tuple-element.23), channel_id=1, source_target_pairs={{0,4},{1,5},{2,6},{3,7},{4,0},{5,1},{6,2},{7,3},{8,12},{9,13},{10,... | collective-permute-start | bytes 258056 | tf_op jit(solution)/shard_map/ppermute | solution.py:81
  9.5 10.1 %collective-permute-start.5 = (bf16[56,768]{1,0:T(8,128)(2,1)}, bf16[56,768]{1,0:T(8,128)(2,1)S(1)}, u32[]{:S(2)}, u32[]{:S(2)}) collective-permute-start(bf16[56,768]{1,0:T(8,128)(2,1)} %get-tuple-element.24), channel_id=1, source_target_pairs={{0,6},{1,7},{2,4},{3,5},{4,2},{5,3},{6,0},{7,1},{8,14},{9,15},{10,... | collective-permute-start | bytes 258056 | tf_op jit(solution)/shard_map/ppermute | solution.py:81
  14.2 6.8 %copy-start.8 = (bf16[56,384]{1,0:T(8,128)(2,1)}, bf16[56,384]{1,0:T(8,128)(2,1)S(1)}, u32[]{:S(2)}) copy-start(bf16[56,384]{1,0:T(8,128)(2,1)S(1)} %collective-permute-done.refs_1_) | copy-start | bytes 129028
  14.2 6.6 %collective-permute-start.2 = (bf16[56,384]{1,0:T(8,128)(2,1)}, bf16[56,384]{1,0:T(8,128)(2,1)S(1)}, u32[]{:S(2)}, u32[]{:S(2)}) collective-permute-start(bf16[56,384]{1,0:T(8,128)(2,1)} %get-tuple-element.20), channel_id=1, source_target_pairs={{0,6},{1,7},{2,4},{3,5},{4,2},{5,3},{6,0},{7,1},{8,14},{9,15},{10,... | collective-permute-start | bytes 129032 | tf_op jit(solution)/shard_map/ppermute | solution.py:81
  14.3 6.7 %copy-start.9 = (bf16[56,384]{1,0:T(8,128)(2,1)}, bf16[56,384]{1,0:T(8,128)(2,1)S(1)}, u32[]{:S(2)}) copy-start(bf16[56,384]{1,0:T(8,128)(2,1)S(1)} %collective-permute-done.1.refs_2_) | copy-start | bytes 129028
  14.3 6.5 %collective-permute-start.6 = (bf16[56,768]{1,0:T(8,128)(2,1)}, bf16[56,768]{1,0:T(8,128)(2,1)S(1)}, u32[]{:S(2)}, u32[]{:S(2)}) collective-permute-start(bf16[56,768]{1,0:T(8,128)(2,1)} %get-tuple-element.21.refs_4_), channel_id=1, source_target_pairs={{0,1},{1,0},{2,3},{3,2},{4,5},{5,4},{6,7},{7,6},{8,9},{9,8},{10,11... | collective-permute-start | bytes 258056 | tf_op jit(solution)/shard_map/ppermute | solution.py:97
  14.4 6.6 %copy-start = (bf16[56,768]{1,0:T(8,128)(2,1)}, bf16[56,768]{1,0:T(8,128)(2,1)S(1)}, u32[]{:S(2)}) copy-start(bf16[56,768]{1,0:T(8,128)(2,1)S(1)} %collective-permute-done.3.refs_5_) | copy-start | bytes 258052
  14.4 6.4 %collective-permute-start.7 = (bf16[56,768]{1,0:T(8,128)(2,1)S(1)}, bf16[56,768]{1,0:T(8,128)(2,1)S(1)}, u32[]{:S(2)}, u32[]{:S(2)}) collective-permute-start(bf16[56,768]{1,0:T(8,128)(2,1)S(1)} %collective-permute-done.3.refs_5_), channel_id=1, source_target_pairs={{0,1},{1,0},{2,3},{3,2},{4,5},{5,4},{6,7},{7,6},{8,9},{9,8},{10,11... | collective-permute-start | bytes 258056 | tf_op jit(solution)/shard_map/ppermute | solution.py:97
  19.5 1.5 %copy-start.1 = (bf16[56,768]{1,0:T(8,128)(2,1)}, bf16[56,768]{1,0:T(8,128)(2,1)S(1)}, u32[]{:S(2)}) copy-start(bf16[56,768]{1,0:T(8,128)(2,1)S(1)} %collective-permute-done.4.refs_6_) | copy-start | bytes 258052
  19.5 1.3 %collective-permute-start.8 = (bf16[56,768]{1,0:T(8,128)(2,1)S(1)}, bf16[56,768]{1,0:T(8,128)(2,1)S(1)}, u32[]{:S(2)}, u32[]{:S(2)}) collective-permute-start(bf16[56,768]{1,0:T(8,128)(2,1)S(1)} %collective-permute-done.4.refs_6_), channel_id=1, source_target_pairs={{0,1},{1,0},{2,3},{3,2},{4,5},{5,4},{6,7},{7,6},{8,9},{9,8},{10,11... | collective-permute-start | bytes 258056 | tf_op jit(solution)/shard_map/ppermute | solution.py:97
  19.5 1.5 %copy-start.2 = (bf16[56,768]{1,0:T(8,128)(2,1)}, bf16[56,768]{1,0:T(8,128)(2,1)S(1)}, u32[]{:S(2)}) copy-start(bf16[56,768]{1,0:T(8,128)(2,1)S(1)} %collective-permute-done.5.refs_7_) | copy-start | bytes 258052
  19.6 1.4 %collective-permute-start.9 = (bf16[56,768]{1,0:T(8,128)(2,1)S(1)}, bf16[56,768]{1,0:T(8,128)(2,1)S(1)}, u32[]{:S(2)}, u32[]{:S(2)}) collective-permute-start(bf16[56,768]{1,0:T(8,128)(2,1)S(1)} %collective-permute-done.5.refs_7_), channel_id=1, source_target_pairs={{0,1},{1,0},{2,3},{3,2},{4,5},{5,4},{6,7},{7,6},{8,9},{9,8},{10,11... | collective-permute-start | bytes 258056 | tf_op jit(solution)/shard_map/ppermute | solution.py:97
  20.8 0.6 %copy-start.10 = (bf16[56,384]{1,0:T(8,128)(2,1)}, bf16[56,384]{1,0:T(8,128)(2,1)S(1)}, u32[]{:S(2)}) copy-start(bf16[56,384]{1,0:T(8,128)(2,1)S(1)} %collective-permute-done.2.refs_3_) | copy-start | bytes 129028
  20.8 0.7 %copy-start.3 = (bf16[56,768]{1,0:T(8,128)(2,1)}, bf16[56,768]{1,0:T(8,128)(2,1)S(1)}, u32[]{:S(2)}) copy-start(bf16[56,768]{1,0:T(8,128)(2,1)S(1)} %collective-permute-done.6.refs_8_) | copy-start | bytes 258052
  20.8 0.7 %copy-start.4 = (bf16[56,768]{1,0:T(8,128)(2,1)}, bf16[56,768]{1,0:T(8,128)(2,1)S(1)}, u32[]{:S(2)}) copy-start(bf16[56,768]{1,0:T(8,128)(2,1)S(1)} %collective-permute-done.7.refs_9_) | copy-start | bytes 258052
  20.8 0.7 %copy-start.5 = (bf16[56,768]{1,0:T(8,128)(2,1)}, bf16[56,768]{1,0:T(8,128)(2,1)S(1)}, u32[]{:S(2)}) copy-start(bf16[56,768]{1,0:T(8,128)(2,1)S(1)} %collective-permute-done.8.refs_10_) | copy-start | bytes 258052
  21.0 0.6 %copy-start.6 = (bf16[56,768]{1,0:T(8,128)(2,1)}, bf16[56,768]{1,0:T(8,128)(2,1)S(1)}, u32[]{:S(2)}) copy-start(bf16[56,768]{1,0:T(8,128)(2,1)S(1)} %collective-permute-done.9.refs_11_) | copy-start | bytes 258052
  24.2 6.1 %collective-permute-start.10 = (bf16[56,384]{1,0:T(8,128)(2,1)}, bf16[56,384]{1,0:T(8,128)(2,1)S(1)}, u32[]{:S(2)}, u32[]{:S(2)}) collective-permute-start(bf16[56,384]{1,0:T(8,128)(2,1)} %get-tuple-element.26), channel_id=1, source_target_pairs={{0,2},{1,3},{2,0},{3,1},{4,6},{5,7},{6,4},{7,5},{8,10},{9,11},{10,... | collective-permute-start | bytes 129032 | tf_op jit(solution)/shard_map/ppermute | solution.py:81
  26.0 6.7 %collective-permute-start.11 = (bf16[56,384]{1,0:T(8,128)(2,1)}, bf16[56,384]{1,0:T(8,128)(2,1)S(1)}, u32[]{:S(2)}, u32[]{:S(2)}) collective-permute-start(bf16[56,384]{1,0:T(8,128)(2,1)} %get-tuple-element.27), channel_id=1, source_target_pairs={{0,4},{1,5},{2,6},{3,7},{4,0},{5,1},{6,2},{7,3},{8,12},{9,13},{10,... | collective-permute-start | bytes 129032 | tf_op jit(solution)/shard_map/ppermute | solution.py:81
  26.2 6.4 %copy-start.7 = (bf16[56,384]{1,0:T(8,128)(2,1)S(1)}, bf16[56,384]{1,0:T(8,128)(2,1)}, u32[]{:S(2)}) copy-start(bf16[56,384]{1,0:T(8,128)(2,1)} %get-tuple-element.25) | copy-start | bytes 129028
  26.2 6.4 %collective-permute-start.12 = (bf16[56,384]{1,0:T(8,128)(2,1)}, bf16[56,384]{1,0:T(8,128)(2,1)S(1)}, u32[]{:S(2)}, u32[]{:S(2)}) collective-permute-start(bf16[56,384]{1,0:T(8,128)(2,1)} %get-tuple-element.28), channel_id=1, source_target_pairs={{0,6},{1,7},{2,4},{3,5},{4,2},{5,3},{6,0},{7,1},{8,14},{9,15},{10,... | collective-permute-start | bytes 129032 | tf_op jit(solution)/shard_map/ppermute | solution.py:81
  43.4 10.9 %copy-start.11 = (f32[1,3072]{1,0:T(1,128)S(1)}, f32[1,3072]{1,0:T(1,128)}, u32[]{:S(2)}) copy-start(f32[1,3072]{1,0:T(1,128)} %param.10) | copy-start | bytes 36868
  44.8 9.4 %all-to-all-start = ((bf16[4,56,768]{2,1,0:T(8,128)(2,1)}), bf16[4,56,768]{2,1,0:T(8,128)(2,1)S(1)}, u32[]{:S(2)}, u32[]{:S(2)}) async-start(bf16[4,56,768]{2,1,0:T(8,128)(2,1)} %bitcast.7), calls=%async_computation | async-start | bytes 688128 | tf_op jit(solution)/shard_map/all_to_all | solution.py:122
